TPU v7x, 32 devices: a whole 2x2x4 slice. The times are simulated.
32 devices in a mesh: leaf: 8 (over y, x, core), sub: 4 (over z).
Axes of the slice: x: 2, y: 2, z: 4, core: 2. Of those that a mesh axis runs over, the one named last changes fastest.
Arguments:
- currents: float32 [65536, 128], P(('leaf', 'sub')), may hold values from -6 to 6
- leaf_basis: float32 [512, 128, 128], P(('leaf', 'sub')), may hold values from -0.5 to 0.5
- leaf_rank: int32 [512], P(('leaf', 'sub')), may hold values from 64 to 128
- leaf_transfer: float32 [512, 128, 128], P(('leaf', 'sub')), may hold values from -0.25 to 0.25
- top_transfer: float32 [8, 4, 128, 128], P('leaf', None, None, 'sub'), may hold values from -0.375 to 0.375
- far_table: float32 [32, 2, 128, 128], replicated, may hold values from -0.125 to 0.125
- send_src: int32 [32, 3, 4, 12], P(('leaf', 'sub')), may hold values from -1 to 15, as said below
- recv_tgt: int32 [32, 3, 4, 12], P(('leaf', 'sub')), may hold values from -1 to 15, as said below
- recv_type: int32 [32, 3, 4, 12], P(('leaf', 'sub')), may hold values from 0 to 31, as said below
- top_coupling: float32 [8, 4, 2, 128, 128], P('leaf', None, None, 'sub'), may hold values from -0.1875 to 0.1875
- top_list: int32 [8, 4], P('leaf'), may hold values from 0 to 7, as said below
- near_blocks: float32 [2048, 2, 128, 128], P(('leaf', 'sub')), may hold values from -0.1875 to 0.1875
- near_tgt: int32 [32, 64], P(('leaf', 'sub')), may hold values from 0 to 15, as said below
- near_src: int32 [32, 64], P(('leaf', 'sub')), may hold values from 0 to 23, as said below
Outputs:
- potential: float32 [65536, 128], P(('leaf', 'sub'))
Inputs may be any that keep to these rules, and one draw needn't show every extreme that they name: `send_src`: entry [q, o, s, j] names the leaf of device q (counted from its first leaf) whose coefficients fill slot j of what device q sends to device (q // 4 + o - 1) * 4 + s, or -1 for an empty slot; it is -1 wherever q // 4 + o - 1 lies outside 0 to 7. In every draw some device receives 12 filled slots from every device of its own group and of the two groups beside it. `recv_tgt`: entry [p, o, s, j] is the leaf of device p (counted from its first leaf) on which slot j from device (p // 4 + o - 1) * 4 + s acts; it is -1 exactly where that slot is empty or that device does not exist. `recv_type`: entry [p, o, s, j] selects the matrix of far_table for slot j from device (p // 4 + o - 1) * 4 + s to device p. `top_list`: row g names 4 different groups, none equal to g. `near_tgt`: counted from the device's first leaf. `near_src`: counted from 4 leaves before the device's first leaf; it lies within 4 leaves of the block's target leaf.
All inputs are finite; a program needn't handle non-finite values.
Results may differ from a plain program's by a relative error of at most 0.0003.
Values sent between devices are 32-bit elements; how exact they have to be, the bound alone decides.
A program may use at most 192 MiB of HBM per device.

v0:
```python
import functools

import jax
import jax.numpy as jnp
from jax import lax
from jax.experimental import pallas as pl
from jax.experimental.pallas import tpu as pltpu
from jax.sharding import PartitionSpec as P

HALO_L = 4
F32 = jnp.float32
BF16 = jnp.bfloat16
NN = (((1,), (0,)), ((), ()))
TN = (((0,), (0,)), ((), ()))

SMEM = pl.BlockSpec(memory_space=pltpu.SMEM)
VMEM = pl.BlockSpec(memory_space=pltpu.VMEM)
ANY = pl.BlockSpec(memory_space=pl.ANY)
MESH = pl.DeviceIdType.MESH


def split(x):
    high = x.astype(BF16)
    return high, (x - high.astype(F32)).astype(BF16)


def dot(a, b, dims=NN):
    return lax.dot_general(a, b, dims, preferred_element_type=F32)


def dot3(a, b, dims=NN):
    ah, al = split(a)
    bh, bl = split(b)
    return dot(ah, bh, dims) + (dot(ah, bl, dims) + dot(al, bh, dims))


def rotated(c):
    half = c.shape[-1] // 2
    lane = lax.broadcasted_iota(jnp.int32, c.shape, c.ndim - 1)
    turned_c = pltpu.roll(c, half, c.ndim - 1)
    return jnp.where(lane < half, -turned_c, turned_c)


def lay_out(store, at, c):
    rows, cols = c.shape
    high, low = split(c)
    rhigh, rlow = split(rotated(c))
    store[at, :rows, :cols] = high
    store[at, :rows, cols:] = low
    store[at, rows:, :cols] = rhigh
    store[at, rows:, cols:] = rlow


def applied(mh, ml, b):
    cols = b.shape[1] // 2
    p = dot(mh, b)
    return p[:, :cols] + (p[:, cols:] + dot(ml, b[:, :cols]))


def masked(basis, rank):
    lane = lax.broadcasted_iota(jnp.int32, basis.shape, 1)
    return jnp.where(lane < rank, basis, 0.0)


CHUNKS = 8
FLIGHT = 2
PARTS = 4
FAR, SECOND, END, OWN = range(4)
NEXT, PREV, SIDE = range(3)


def ordered(tgt, src, kind, count, leaves, spare):
    rows = -(-count // 8) * 8
    lane = lax.broadcasted_iota(jnp.int32, (rows, 128), 1)
    line = lax.broadcasted_iota(jnp.int32, (rows, 128), 0)
    spot = lax.broadcasted_iota(jnp.int32, (1, 128), 1)
    src = jnp.where(tgt < 0, spare, src).astype(F32)
    key = jnp.where(tgt < 0, leaves, tgt)
    key = jnp.where(spot < count, key, leaves + 1).astype(F32)
    stood = lambda x: jnp.sum(jnp.where(line == lane, x, 0.0), axis=1, keepdims=True)
    key_at = stood(key)
    before = (key < key_at) | ((key == key_at) & (lane < line))
    place = jnp.sum(jnp.where(before, 1.0, 0.0), axis=1, keepdims=True)
    hot = (place == lane.astype(F32)) & (line < count)
    pick = lambda x: jnp.sum(jnp.where(hot, stood(x), 0.0), axis=0, keepdims=True)
    key, src, kind = pick(key), pick(src), pick(kind.astype(F32))
    wide = jnp.broadcast_to(key, (8, 128))
    keep = jnp.where((wide == pltpu.roll(wide, 1, 1))[:1] & (spot > 0), 1.0, 0.0)
    wide = (leaves, 128)
    lane = lax.broadcasted_iota(jnp.int32, wide, 1)
    line = lax.broadcasted_iota(jnp.int32, wide, 0)
    found = (key == line.astype(F32)) & (lane < count)
    last = jnp.max(jnp.where(found, lane.astype(F32), -1.0), axis=1, keepdims=True)
    last = jnp.sum(jnp.where(line == lane, last, 0.0), axis=0, keepdims=True)
    return [x.astype(jnp.int32) for x in (src, kind, keep, last)]


def within(i, ref):
    return jnp.clip(i, 0, ref.shape[0] - 1)


def field_kernel(
    slots_count,
    partner,
    rank,
    send_src,
    recv_tgt,
    recv_type,
    near_tgt,
    near_src,
    shares,
    coupling,
    cur_in,
    basis_in,
    transfer_in,
    blocks_in,
    table_in,
    out,
    cur,
    basis,
    transfer,
    blocks,
    table,
    high,
    low,
    coef,
    raw,
    ext_in,
    rim,
    laid,
    laid_ext,
    runs,
    part,
    from_end,
    from_other,
    near_part,
    whole,
    mid,
    top_part,
    top_in,
    top_own,
    tops,
    field_own,
    numbers,
    sources,
    sub_in,
    src_in,
    src_sum,
    ext_src,
    near_rows,
    far_rows,
    near_slots,
    slots,
    load_sem,
    block_sem,
    table_sem,
    rows_sem,
    rim_sem,
    number_sem,
    source_sem,
    ext_src_sem,
    raw_sem,
    ext_sem,
    whole_sem,
    share_sem,
    top_sem,
    all_sem,
    field_sem,
    out_sem,
    end_sem,
    other_sem,
    back_sem,
):
    n = lax.axis_size("sub")
    groups = lax.axis_size("leaf")
    me = lax.axis_index("sub")
    group = lax.axis_index("leaf")
    leaves = cur.shape[0]
    halo = rim.shape[1]
    count = slots_count
    near_count = blocks.shape[0]
    per = leaves // CHUNKS
    up_per = leaves // PARTS
    share = whole.shape[0] // n
    low_side = me < n // 2
    is_end = (me == 0) | (me == n - 1)
    is_inner = (me != 0) & (me != n - 1)
    end = jnp.where(low_side, 0, n - 1)
    inner = jnp.where(low_side, 1, n - 2)
    other = n - 1 - inner
    has_up = group + 1 < groups
    has_down = group > 0
    has_after = has_up | (me < n - 1)
    has_before = has_down | (me > 0)
    up_group = jnp.minimum(group + 1, groups - 1)
    down_group = jnp.maximum(group - 1, 0)
    after = (jnp.where(me < n - 1, group, up_group), lax.rem(me + 1, n))
    before = (jnp.where(me > 0, group, down_group), lax.rem(me + n - 1, n))

    barrier = pltpu.get_barrier_semaphore()

    def greet(device):
        pl.semaphore_signal(barrier, inc=1, device_id=device, device_id_type=MESH)

    for d in range(1, n):
        greet((group, lax.rem(me + d, n)))
    for d in range(1, groups):
        greet((lax.rem(group + d, groups), me))
    cross_after = (me == n - 1) & has_up
    cross_before = (me == 0) & has_down

    @pl.when(cross_after)
    def _():
        greet(after)

    @pl.when(cross_before)
    def _():
        greet(before)

    def up_chunk(p):
        return pl.ds(p * up_per, up_per)

    def load(i, p):
        source, target = ((cur_in, cur), (basis_in, basis), (transfer_in, transfer))[i]
        return pltpu.make_async_copy(
            source.at[up_chunk(p)], target.at[up_chunk(p)], load_sem.at[i, p]
        )

    for p in range(PARTS):
        for i in range(3):
            load(i, p).start()

    def block_load(p):
        span = pl.ds(p * (near_count // PARTS), near_count // PARTS)
        return pltpu.make_async_copy(blocks_in.at[span], blocks.at[span], block_sem.at[p])

    def table_load(p):
        span = pl.ds(p * (table.shape[0] // PARTS), table.shape[0] // PARTS)
        return pltpu.make_async_copy(table_in.at[span], table.at[span], table_sem.at[p])

    for p in range(PARTS):
        block_load(p).start()
    for p in range(PARTS):
        table_load(p).start()

    cap = send_src.shape[2]
    padded = lambda *parts: jnp.concatenate(
        [*parts, jnp.zeros((parts[0].shape[0], 128 - sum(x.shape[1] for x in parts)), jnp.int32)],
        axis=1,
    )
    triple = lambda ref: padded(*(ref[o] for o in range(3)))
    numbers[:n, :] = triple(recv_tgt)
    numbers[n:, :] = triple(recv_type)
    sources[:n, :] = triple(send_src)
    sources[n:, :] = jnp.zeros((8 - n, 128), jnp.int32)
    near_kind = lax.broadcasted_iota(jnp.int32, (1, 128), 1)
    for i, row in enumerate(
        ordered(padded(near_tgt[...]), padded(near_src[...]), near_kind, near_count, leaves, 0)
    ):
        near_rows[i : i + 1, :] = row
    near_copy = pltpu.make_async_copy(near_rows, near_slots, rows_sem.at[0])

    pl.semaphore_wait(
        barrier, n + groups - 2 + jnp.where(cross_after, 1, 0) + jnp.where(cross_before, 1, 0)
    )
    near_copy.start()

    def remote(source, target, sems, at, device):
        return pltpu.make_async_remote_copy(
            src_ref=source,
            dst_ref=target,
            send_sem=sems.at[(0, *at)],
            recv_sem=sems.at[(1, *at)],
            device_id=device,
            device_id_type=MESH,
        )

    def sub_peer(d):
        return (group, lax.rem(me + d, n))

    def rim_copy(side):
        if side == 0:
            return remote(cur_in.at[pl.ds(leaves - halo, halo)], rim.at[0], rim_sem, (0,), after)
        return remote(cur_in.at[pl.ds(0, halo)], rim.at[1], rim_sem, (1,), before)

    sends_rim = [has_after, has_before]
    takes_rim = [has_before, has_after]
    for side in range(2):
        @pl.when(sends_rim[side])
        def _(side=side):
            rim_copy(side).start()

        @pl.when(jnp.logical_not(takes_rim[side]))
        def _(side=side):
            rim[side] = jnp.zeros(rim.shape[1:], F32)

    def number_copy(d):
        return remote(
            numbers, sub_in.at[me], number_sem, (d - 1,), sub_peer(d)
        )

    def whole_copy(d):
        mine = pl.ds(pl.multiple_of(me * share, share), share)
        return remote(
            shares.at[lax.rem(me + d, n)], whole.at[mine], whole_sem, (d - 1,), sub_peer(d)
        )

    for d in range(1, n):
        number_copy(d).start()
        whole_copy(d).start()

    def source_copy(side):
        there = (up_group, me) if side == 0 else (down_group, me)
        return remote(sources, src_in.at[side], source_sem, (side,), there)

    sends_leaf = [has_up, has_down]
    takes_leaf = [has_down, has_up]
    for side in range(2):
        @pl.when(sends_leaf[side])
        def _(side=side):
            source_copy(side).start()

        @pl.when(jnp.logical_not(takes_leaf[side]))
        def _(side=side):
            src_in[side] = jnp.zeros(src_in.shape[1:], jnp.int32)
            raw[side] = jnp.zeros(raw.shape[1:], F32)

    def raw_copy(to, p):
        there = {NEXT: (up_group, me), PREV: (down_group, me), SIDE: (group, inner)}[to]
        return remote(coef.at[up_chunk(p)], raw.at[to, up_chunk(p)], raw_sem, (to, p), there)

    sends_raw = [has_up, has_down, is_end]
    takes_raw = [has_down, has_up, is_inner]

    def send_raw(p):
        for to in range(3):
            @pl.when(sends_raw[to])
            def _(to=to):
                raw_copy(to, p).start()

    total = jnp.zeros(mid.shape, F32)
    for p in range(PARTS):
        for i in range(3):
            load(i, p).wait()
        for i in range(up_per):
            l = p * up_per + i
            c = dot3(masked(basis[l], rank[l]), cur[l], TN)
            coef[l] = c
            total += dot3(transfer[l], c, TN)
        if p:
            send_raw(p - 1)
    mid[...] = total
    mine = pl.ds(pl.multiple_of(me * share, share), share)
    whole[mine, :] = shares[me]
    for d in range(1, n):
        whole_copy(d).wait_recv()
    send_raw(PARTS - 1)
    top_part[...] = dot3(whole[...], mid[...])

    for side in range(2):
        @pl.when(takes_rim[side])
        def _(side=side):
            rim_copy(side).wait_recv()

    def share_copy(d):
        there = lax.rem(me + d, n)
        span = pl.ds(pl.multiple_of(there * share, share), share)
        return remote(top_part.at[span], top_in.at[me], share_sem, (d - 1,), sub_peer(d))

    @pl.loop(0, halo)
    def _(l):
        lay_out(laid_ext, l, rim[0, l])
        lay_out(laid_ext, halo + leaves + l, rim[1, l])

    @pl.loop(0, leaves, unroll=2)
    def _(l):
        lay_out(laid_ext, halo + l, cur[l])

    for d in range(1, n):
        share_copy(d).start()

    def gather(rows, at, store):
        @pl.loop(0, leaves, unroll=2)
        def _(l):
            j = rows[4 * at + 3, l]
            store(l, runs[within(j, runs)] * jnp.where(j >= 0, 1.0, 0.0))

    def in_order(rows, at, number, product):
        unroll = max(u for u in range(1, 7) if number % u == 0)

        def step(i, acc):
            spots = [i * unroll + u for u in range(unroll)]
            results = [product(rows[4 * at, j], rows[4 * at + 1, j]) for j in spots]
            for j, result in zip(spots, results):
                acc = acc * rows[4 * at + 2, j].astype(F32) + result
                runs[j] = acc
            return acc

        lax.fori_loop(0, number // unroll, step, jnp.zeros(runs.shape[1:], F32))

    def near_product(s, k):
        k = within(k, blocks)
        h0, l0 = split(blocks[k, 0])
        h1, l1 = split(blocks[k, 1])
        b = laid_ext[within(s, laid_ext)]
        return applied(jnp.concatenate([h0, h1], axis=1), jnp.concatenate([l0, l1], axis=1), b)

    def put_near(l, value):
        near_part[l] = value

    near_copy.wait()
    for p in range(PARTS):
        block_load(p).wait()
    in_order(near_slots, 0, near_count, near_product)
    gather(near_slots, 0, put_near)

    top_in[me] = top_part[mine, :]
    for d in range(1, n):
        share_copy(d).wait_recv()
    total = top_in[0]
    for s in range(1, n):
        total += top_in[s]
    top_own[mine, :] = total

    for side in range(2):
        @pl.when(takes_leaf[side])
        def _(side=side):
            source_copy(side).wait_recv()

    spot = lax.broadcasted_iota(jnp.int32, (8, 128), 1)
    src_sum[...] = jnp.where(
        spot < cap,
        pltpu.roll(src_in[0], 128 - 2 * cap, 1),
        jnp.where(
            spot < 2 * cap, sources[...] + leaves, pltpu.roll(src_in[1], 2 * cap, 1) + 2 * leaves
        ),
    )

    for p in range(PARTS):
        table_load(p).wait()

    @pl.loop(0, table.shape[0])
    def _(i):
        w = table.shape[3]
        h0, l0 = split(table[i, 0])
        h1, l1 = split(table[i, 1])
        high[i, :, :w] = h0
        high[i, :, w:] = h1
        low[i, :, :w] = l0
        low[i, :, w:] = l1

    def top_copy(d):
        return remote(top_own.at[mine], top_own.at[mine], top_sem, (d - 1,), sub_peer(d))

    for d in range(1, n):
        top_copy(d).start()

    ext_src_copy = remote(src_sum, ext_src, ext_src_sem, (), (group, inner))

    @pl.when(is_end)
    def _():
        ext_src_copy.start()
        ext_src[...] = jnp.zeros(ext_src.shape, jnp.int32)

    @pl.loop(0, leaves, unroll=2)
    def _(l):
        lay_out(laid, leaves + l, coef[l])

    sub_in[me] = numbers[...]
    for d in range(1, n):
        number_copy(d).wait_recv()

    @pl.when(is_inner)
    def _():
        ext_src_copy.wait_recv()

    for s in range(n + 1):
        if s < n:
            args = sub_in[s, pl.ds(me, 1)], src_sum[s : s + 1], sub_in[s, pl.ds(n + me, 1)]
        else:
            args = numbers[pl.ds(end, 1)], ext_src[pl.ds(me, 1)], numbers[pl.ds(n + end, 1)]
        for i, row in enumerate(ordered(*args, count, leaves, leaves)):
            far_rows[4 * s + i : 4 * s + i + 1, :] = row
    far_copy = pltpu.make_async_copy(far_rows, slots, rows_sem.at[1])

    for to in (NEXT, PREV):
        @pl.when(takes_raw[to])
        def _(to=to):
            for p in range(PARTS):
                raw_copy(to, p).wait_recv()

    far_copy.start()

    @pl.loop(0, leaves, unroll=2)
    def _(l):
        lay_out(laid, l, raw[NEXT, l])
        lay_out(laid, 2 * leaves + l, raw[PREV, l])

    far_copy.wait()

    def compute(at, store, role, add=False):
        def product(s, k):
            k = within(k, high)
            return applied(high[k], low[k], store[within(s, store)])

        in_order(slots, at, count, product)

        def put(l, value):
            part[role, l] = part[role, l] + value if add else value

        gather(slots, at, put)

    def chunk(c):
        return pl.ds(c * per, per)

    def end_copy(role, c):
        return pltpu.make_async_remote_copy(
            src_ref=part.at[role, chunk(c)],
            dst_ref=from_end.at[role, chunk(c)],
            send_sem=out_sem.at[role, c],
            recv_sem=end_sem.at[role, c],
            device_id=(group, inner),
            device_id_type=MESH,
        )

    def other_copy(role, c):
        return pltpu.make_async_remote_copy(
            src_ref=part.at[role, chunk(c)],
            dst_ref=from_other.at[role, chunk(c)],
            send_sem=out_sem.at[role, c],
            recv_sem=other_sem.at[role, c],
            device_id=(group, other),
            device_id_type=MESH,
        )

    def back_copy(c):
        return pltpu.make_async_remote_copy(
            src_ref=part.at[END, chunk(c)],
            dst_ref=from_other.at[1, chunk(c)],
            send_sem=back_sem.at[c],
            recv_sem=other_sem.at[1, c],
            device_id=(group, end),
            device_id_type=MESH,
        )

    def relay(role, c):
        @pl.when(is_inner)
        def _():
            end_copy(role, c).wait_recv()
            part[role, chunk(c)] += from_end[role, chunk(c)]
            other_copy(role, c).start()

    def relay_back(c):
        @pl.when(is_inner)
        def _():
            other_copy(0, c).wait_recv()
            part[END, chunk(c)] += from_other[0, chunk(c)]
            back_copy(c).start()

    items = [(role, c) for role in (FAR, SECOND) for c in range(CHUNKS)]
    pumped = [0]

    def pump(upto):
        upto = min(upto, len(items))

        @pl.when(is_end)
        def _():
            for i in range(pumped[0], upto):
                if i >= FLIGHT:
                    end_copy(*items[i - FLIGHT]).wait_send()
                end_copy(*items[i]).start()

        pumped[0] = upto

    compute(n - 1 - end, laid, FAR)
    pump(FLIGHT)
    compute(other, laid, SECOND)
    pump(FLIGHT + 1)

    def ext_copy(side):
        there = (up_group, me) if side == 0 else (down_group, me)
        return remote(raw.at[SIDE], ext_in.at[side], ext_sem, (side,), there)

    sends_ext = [is_inner & has_up, is_inner & has_down]
    takes_ext = [is_inner & has_down, is_inner & has_up]

    def all_copy(d):
        return remote(
            top_own, tops.at[group], all_sem, (d - 1,), (lax.rem(group + d, groups), me)
        )

    for d in range(1, n):
        top_copy(d).wait_recv()
    for d in range(1, groups):
        all_copy(d).start()
    tops[group] = top_own[...]

    @pl.when(is_inner)
    def _():
        for p in range(PARTS):
            raw_copy(SIDE, p).wait_recv()

    for side in range(2):
        @pl.when(sends_ext[side])
        def _(side=side):
            ext_copy(side).start()

    @pl.when(is_inner)
    def _():
        compute(end, laid, END)

    pump(FLIGHT + 2)
    relay(FAR, 0)
    compute(me, laid, OWN)
    pump(FLIGHT + 3)
    relay(FAR, 1)
    pump(FLIGHT + 4)
    relay(FAR, 2)
    relay_back(0)
    pump(FLIGHT + 5)
    relay(FAR, 3)
    relay_back(1)
    pump(FLIGHT + 6)

    for d in range(1, groups):
        all_copy(d).wait_recv()
    field = jnp.zeros((share, mid.shape[1]), F32)
    for k in range(partner.shape[0]):
        p = tops[within(partner[k], tops)]
        field += dot3(coupling[k, 0], p) + dot3(coupling[k, 1], rotated(p))
    field_own[mine, :] = field

    def field_copy(d):
        return remote(field_own.at[mine], field_own.at[mine], field_sem, (d - 1,), sub_peer(d))

    relay(FAR, 4)
    relay_back(2)
    for d in range(1, n):
        field_copy(d).start()
    pump(FLIGHT + 7)
    relay(FAR, 5)
    relay_back(3)
    pump(FLIGHT + 8)
    relay(FAR, 6)
    relay_back(4)
    pump(FLIGHT + 9)
    relay(FAR, 7)
    relay_back(5)
    pump(FLIGHT + 10)

    for d in range(1, n):
        field_copy(d).wait_recv()
    mid[...] = dot3(whole[...], field_own[...], TN)

    @pl.loop(0, leaves, unroll=2)
    def _(l):
        part[OWN, l] += dot3(transfer[l], mid[...])

    relay(SECOND, 0)
    relay_back(6)
    pump(FLIGHT + 11)

    def lay_ext(to, at, ref):
        @pl.loop(0, leaves, unroll=2)
        def _(l):
            lay_out(laid_ext, at * leaves + l, ref[to, l])

    @pl.when(is_inner)
    def _():
        lay_ext(SIDE, 1, raw)

    relay(SECOND, 1)
    relay_back(7)
    pump(FLIGHT + 12)
    for side in range(2):
        @pl.when(takes_ext[side])
        def _(side=side):
            ext_copy(side).wait_recv()
            lay_ext(side, 2 * side, ext_in)

    relay(SECOND, 2)
    pump(FLIGHT + 13)

    @pl.when(is_inner)
    def _():
        compute(n, laid_ext, OWN, add=True)

    def finish(c):
        other_copy(1, c).wait_recv()
        for i in range(per):
            l = c * per + i
            field = part[OWN, l] + from_other[1, l]
            out[l] = dot3(masked(basis[l], rank[l]), field) + near_part[l]

    relay(SECOND, 3)
    pump(FLIGHT + 14)
    done = 0
    for c in range(4, CHUNKS + 2):
        if c < CHUNKS:
            relay(SECOND, c)
        while done <= c - 2:
            finish(done)
            done += 1

    for side in range(2):
        @pl.when(sends_rim[side])
        def _(side=side):
            rim_copy(side).wait_send()

        @pl.when(sends_leaf[side])
        def _(side=side):
            source_copy(side).wait_send()

        @pl.when(sends_ext[side])
        def _(side=side):
            ext_copy(side).wait_send()

    for to in range(3):
        @pl.when(sends_raw[to])
        def _(to=to):
            for p in range(PARTS):
                raw_copy(to, p).wait_send()

    for d in range(1, n):
        number_copy(d).wait_send()
        whole_copy(d).wait_send()
        share_copy(d).wait_send()
        top_copy(d).wait_send()
        field_copy(d).wait_send()
    for d in range(1, groups):
        all_copy(d).wait_send()

    @pl.when(is_inner)
    def _():
        for c in range(CHUNKS):
            other_copy(FAR, c).wait_send()
            other_copy(SECOND, c).wait_send()
            back_copy(c).wait_send()

    @pl.when(is_end)
    def _():
        ext_src_copy.wait_send()
        for item in items[-FLIGHT:]:
            end_copy(*item).wait_send()


def fields(count, partner, rank, numbers, shares, coupling, cur, basis, transfer, blocks, table):
    leaves, width, cols = cur.shape
    kinds = table.shape[0]
    n = lax.axis_size("sub")
    groups = lax.axis_size("leaf")
    share = width // n
    f32 = lambda *shape: pltpu.VMEM(shape, F32)
    i32 = lambda *shape: pltpu.VMEM(shape, jnp.int32)
    b16 = lambda *shape: pltpu.VMEM(shape, BF16)
    block = lambda *lead: f32(*lead, width, cols)
    dma = lambda *shape: pltpu.SemaphoreType.DMA(shape)
    lists = 4 * (n + 1)
    lists = -(-lists // 8) * 8
    return pl.pallas_call(
        functools.partial(field_kernel, count),
        in_specs=[SMEM] * 2 + [VMEM] * 7 + [ANY] * 5,
        out_specs=VMEM,
        out_shape=jax.ShapeDtypeStruct((leaves, width, cols), F32),
        scratch_shapes=[
            block(leaves),
            f32(*basis.shape),
            f32(*transfer.shape),
            f32(*blocks.shape),
            f32(*table.shape),
            b16(kinds, width, 2 * width),
            b16(kinds, width, 2 * width),
            block(leaves),
            block(3, leaves),
            block(2, leaves),
            block(2, HALO_L),
            b16(3 * leaves, 2 * width, 2 * cols),
            b16(3 * leaves, 2 * width, 2 * cols),
            block(max(count, blocks.shape[0])),
            block(4, leaves),
            block(2, leaves),
            block(2, leaves),
            block(leaves),
            f32(width, width),
            block(),
            block(),
            f32(n, share, cols),
            block(),
            block(groups),
            block(),
            i32(2 * n, 128),
            i32(8, 128),
            i32(n, 2 * n, 128),
            i32(2, 8, 128),
            i32(8, 128),
            i32(8, 128),
            i32(8, 128),
            i32(lists, 128),
            pltpu.SMEM((8, 128), jnp.int32),
            pltpu.SMEM((lists, 128), jnp.int32),
            dma(3, PARTS),
            dma(PARTS),
            dma(PARTS),
            dma(2),
            dma(2, 2),
            dma(2, n - 1),
            dma(2, 2),
            dma(2),
            dma(2, 3, PARTS),
            dma(2, 2),
            dma(2, n - 1),
            dma(2, n - 1),
            dma(2, n - 1),
            dma(2, groups - 1),
            dma(2, n - 1),
            dma(2, CHUNKS),
            dma(2, CHUNKS),
            dma(2, CHUNKS),
            dma(CHUNKS),
        ],
        compiler_params=pltpu.CompilerParams(
            vmem_limit_bytes=67043328, collective_id=0, has_side_effects=True
        ),
        cost_estimate=pl.CostEstimate(
            flops=int(9 * count * 12 * width * width * cols),
            bytes_accessed=20 * 2 ** 20,
            transcendentals=0,
        ),
        name="fields",
    )(partner, rank, *numbers, shares, coupling, cur, basis, transfer, blocks, table)


def per_device(
    currents,
    leaf_basis,
    leaf_rank,
    leaf_transfer,
    top_transfer,
    far_table,
    send_src,
    recv_tgt,
    recv_type,
    top_coupling,
    top_list,
    near_blocks,
    near_tgt,
    near_src,
):
    leaves, panel, _ = leaf_basis.shape
    cols = currents.shape[1]
    out = fields(
        3 * send_src.shape[3],
        top_list[0],
        leaf_rank,
        [send_src[0], recv_tgt[0], recv_type[0], near_tgt, near_src],
        jnp.swapaxes(top_transfer[0], 1, 2),
        top_coupling[0],
        currents.reshape(leaves, panel, cols),
        leaf_basis,
        leaf_transfer,
        near_blocks,
        far_table,
    )
    return out.reshape(leaves * panel, cols)


def solution(mesh):
    placed = (
        P(("leaf", "sub"), None),
        P(("leaf", "sub"), None, None),
        P(("leaf", "sub")),
        P(("leaf", "sub"), None, None),
        P("leaf", None, None, "sub"),
        P(),
        P(("leaf", "sub"), None, None, None),
        P(("leaf", "sub"), None, None, None),
        P(("leaf", "sub"), None, None, None),
        P("leaf", None, None, "sub", None),
        P("leaf", None),
        P(("leaf", "sub"), None, None, None),
        P(("leaf", "sub"), None),
        P(("leaf", "sub"), None),
    )
    return jax.shard_map(
        per_device, mesh=mesh, in_specs=placed, out_specs=P(("leaf", "sub"), None), check_vma=False
    )
```

profile of v0, /device:TPU:14, one launch (start us, length us, event | category | flops | bytes accessed | tf_op | source)
XLA Modules:
  0.0 108.9 jit_solution(13049448908488321549)
XLA Ops:
  0.0 106.6 %fields.1 = f32[16,128,128]{2,1,0:T(8,128)} custom-call(s32[4]{0:T(128)} %bitcast.17, s32[16]{0:T(128)} %rank.1, s32[3,4,12]{2,1,0:T(4,128)} %bitcast.14, s32[3,4,12]{2,1,0:T(4,128)} %bitcast.15, s32[3,4,12]{2,1,0:T(4,128)} %bitcast.16, s32[1,64]{1,0:T(1,128)} %near_tgt.1, s32[1,64]{1,0:T(1,128)} %near_src.1, f32[4,32,128]{2,1,0:T(8,128)} %bitcast.13, ...), custom_call_target="tpu_custom_call" | custom-call | flops 8153726976 | bytes 20971520 | tf_op jit(solution)/shard_map/fields/pallas_call | solution.py:760
  106.6 2.3 %copy.16 = f32[2048,128]{1,0:T(8,128)} copy(f32[2048,128]{1,0:T(8,128)} %bitcast.10) | data formatting | bytes 2097152
where the time goes:
time: 109 us
  Pallas kernels  107 us (98%)
  local copies, waits for them, and re-layouts  2.26 us (2%)
    pallas_call x1, Pallas kernels, fields(): pl.pallas_call(functools.partial(field_kernel, count), in_specs=[SMEM] *...  107 us
    unnamed x1, local copies, waits for them, and re-layouts  2.26 us

commit v1 on v0

--- a/solution.py
+++ b/solution.py
@@ -64,6 +64,7 @@
 
 CHUNKS = 8
 FLIGHT = 2
+AHEAD = 2
 PARTS = 4
 FAR, SECOND, END, OWN = range(4)
 NEXT, PREV, SIDE = range(3)
@@ -129,6 +130,7 @@
     rim,
     laid,
     laid_ext,
+    laid_near,
     runs,
     part,
     from_end,
@@ -149,8 +151,10 @@
     ext_src,
     near_rows,
     far_rows,
+    ext_rows,
     near_slots,
     slots,
+    ext_slots,
     load_sem,
     block_sem,
     table_sem,
@@ -283,17 +287,6 @@
             return remote(cur_in.at[pl.ds(leaves - halo, halo)], rim.at[0], rim_sem, (0,), after)
         return remote(cur_in.at[pl.ds(0, halo)], rim.at[1], rim_sem, (1,), before)
 
-    sends_rim = [has_after, has_before]
-    takes_rim = [has_before, has_after]
-    for side in range(2):
-        @pl.when(sends_rim[side])
-        def _(side=side):
-            rim_copy(side).start()
-
-        @pl.when(jnp.logical_not(takes_rim[side]))
-        def _(side=side):
-            rim[side] = jnp.zeros(rim.shape[1:], F32)
-
     def number_copy(d):
         return remote(
             numbers, sub_in.at[me], number_sem, (d - 1,), sub_peer(d)
@@ -324,6 +317,18 @@
         def _(side=side):
             src_in[side] = jnp.zeros(src_in.shape[1:], jnp.int32)
             raw[side] = jnp.zeros(raw.shape[1:], F32)
+
+    sends_rim = [has_after, has_before]
+    takes_rim = [has_before, has_after]
+    late_rim = [me == 0, me == n - 1]
+    for side in range(2):
+        @pl.when(sends_rim[side] & jnp.logical_not(late_rim[side]))
+        def _(side=side):
+            rim_copy(side).start()
+
+        @pl.when(jnp.logical_not(takes_rim[side]))
+        def _(side=side):
+            rim[side] = jnp.zeros(rim.shape[1:], F32)
 
     def raw_copy(to, p):
         there = {NEXT: (up_group, me), PREV: (down_group, me), SIDE: (group, inner)}[to]
@@ -357,24 +362,10 @@
     send_raw(PARTS - 1)
     top_part[...] = dot3(whole[...], mid[...])
 
-    for side in range(2):
-        @pl.when(takes_rim[side])
-        def _(side=side):
-            rim_copy(side).wait_recv()
-
     def share_copy(d):
         there = lax.rem(me + d, n)
         span = pl.ds(pl.multiple_of(there * share, share), share)
         return remote(top_part.at[span], top_in.at[me], share_sem, (d - 1,), sub_peer(d))
-
-    @pl.loop(0, halo)
-    def _(l):
-        lay_out(laid_ext, l, rim[0, l])
-        lay_out(laid_ext, halo + leaves + l, rim[1, l])
-
-    @pl.loop(0, leaves, unroll=2)
-    def _(l):
-        lay_out(laid_ext, halo + l, cur[l])
 
     for d in range(1, n):
         share_copy(d).start()
@@ -402,25 +393,11 @@
         k = within(k, blocks)
         h0, l0 = split(blocks[k, 0])
         h1, l1 = split(blocks[k, 1])
-        b = laid_ext[within(s, laid_ext)]
+        b = laid_near[within(s, laid_near)]
         return applied(jnp.concatenate([h0, h1], axis=1), jnp.concatenate([l0, l1], axis=1), b)
 
     def put_near(l, value):
         near_part[l] = value
-
-    near_copy.wait()
-    for p in range(PARTS):
-        block_load(p).wait()
-    in_order(near_slots, 0, near_count, near_product)
-    gather(near_slots, 0, put_near)
-
-    top_in[me] = top_part[mine, :]
-    for d in range(1, n):
-        share_copy(d).wait_recv()
-    total = top_in[0]
-    for s in range(1, n):
-        total += top_in[s]
-    top_own[mine, :] = total
 
     for side in range(2):
         @pl.when(takes_leaf[side])
@@ -449,12 +426,6 @@
         low[i, :, :w] = l0
         low[i, :, w:] = l1
 
-    def top_copy(d):
-        return remote(top_own.at[mine], top_own.at[mine], top_sem, (d - 1,), sub_peer(d))
-
-    for d in range(1, n):
-        top_copy(d).start()
-
     ext_src_copy = remote(src_sum, ext_src, ext_src_sem, (), (group, inner))
 
     @pl.when(is_end)
@@ -470,18 +441,15 @@
     for d in range(1, n):
         number_copy(d).wait_recv()
 
-    @pl.when(is_inner)
-    def _():
-        ext_src_copy.wait_recv()
-
-    for s in range(n + 1):
-        if s < n:
-            args = sub_in[s, pl.ds(me, 1)], src_sum[s : s + 1], sub_in[s, pl.ds(n + me, 1)]
-        else:
-            args = numbers[pl.ds(end, 1)], ext_src[pl.ds(me, 1)], numbers[pl.ds(n + end, 1)]
+    def put_rows(at, rows, args):
         for i, row in enumerate(ordered(*args, count, leaves, leaves)):
-            far_rows[4 * s + i : 4 * s + i + 1, :] = row
+            rows[4 * at + i : 4 * at + i + 1, :] = row
+
+    for s in range(n):
+        args = sub_in[s, pl.ds(me, 1)], src_sum[s : s + 1], sub_in[s, pl.ds(n + me, 1)]
+        put_rows(s, far_rows, args)
     far_copy = pltpu.make_async_copy(far_rows, slots, rows_sem.at[1])
+    ext_copy_rows = pltpu.make_async_copy(ext_rows, ext_slots, rows_sem.at[2])
 
     for to in (NEXT, PREV):
         @pl.when(takes_raw[to])
@@ -498,27 +466,27 @@
 
     far_copy.wait()
 
-    def compute(at, store, role, add=False):
+    def compute(rows, at, store, role, add=False):
         def product(s, k):
             k = within(k, high)
             return applied(high[k], low[k], store[within(s, store)])
 
-        in_order(slots, at, count, product)
+        in_order(rows, at, count, product)
 
         def put(l, value):
             part[role, l] = part[role, l] + value if add else value
 
-        gather(slots, at, put)
+        gather(rows, at, put)
 
     def chunk(c):
         return pl.ds(c * per, per)
 
-    def end_copy(role, c):
+    def end_copy(c):
         return pltpu.make_async_remote_copy(
-            src_ref=part.at[role, chunk(c)],
-            dst_ref=from_end.at[role, chunk(c)],
-            send_sem=out_sem.at[role, c],
-            recv_sem=end_sem.at[role, c],
+            src_ref=part.at[FAR, chunk(c)],
+            dst_ref=from_end.at[chunk(c)],
+            send_sem=out_sem.at[FAR, c],
+            recv_sem=end_sem.at[c],
             device_id=(group, inner),
             device_id_type=MESH,
         )
@@ -543,12 +511,12 @@
             device_id_type=MESH,
         )
 
-    def relay(role, c):
+    def relay(c):
         @pl.when(is_inner)
         def _():
-            end_copy(role, c).wait_recv()
-            part[role, chunk(c)] += from_end[role, chunk(c)]
-            other_copy(role, c).start()
+            end_copy(c).wait_recv()
+            part[FAR, chunk(c)] += from_end[chunk(c)]
+            other_copy(FAR, c).start()
 
     def relay_back(c):
         @pl.when(is_inner)
@@ -557,25 +525,20 @@
             part[END, chunk(c)] += from_other[0, chunk(c)]
             back_copy(c).start()
 
-    items = [(role, c) for role in (FAR, SECOND) for c in range(CHUNKS)]
     pumped = [0]
 
     def pump(upto):
-        upto = min(upto, len(items))
-
         @pl.when(is_end)
         def _():
-            for i in range(pumped[0], upto):
-                if i >= FLIGHT:
-                    end_copy(*items[i - FLIGHT]).wait_send()
-                end_copy(*items[i]).start()
+            for c in range(pumped[0], upto):
+                if c >= FLIGHT:
+                    end_copy(c - FLIGHT).wait_send()
+                end_copy(c).start()
 
         pumped[0] = upto
 
-    compute(n - 1 - end, laid, FAR)
+    compute(slots, n - 1 - end, laid, FAR)
     pump(FLIGHT)
-    compute(other, laid, SECOND)
-    pump(FLIGHT + 1)
 
     def ext_copy(side):
         there = (up_group, me) if side == 0 else (down_group, me)
@@ -589,39 +552,96 @@
             top_own, tops.at[group], all_sem, (d - 1,), (lax.rem(group + d, groups), me)
         )
 
+    def lay_ext(to, at, ref):
+        @pl.loop(0, leaves, unroll=2)
+        def _(l):
+            lay_out(laid_ext, at * leaves + l, ref[to, l])
+
+    @pl.when(is_inner)
+    def _():
+        for p in range(PARTS):
+            raw_copy(SIDE, p).wait_recv()
+
+    for side in range(2):
+        @pl.when(sends_ext[side])
+        def _(side=side):
+            ext_copy(side).start()
+
+    @pl.when(is_inner)
+    def _():
+        compute(slots, other, laid, SECOND)
+        compute(slots, end, laid, END)
+
+    pump(FLIGHT + 1)
+    relay(0)
+    compute(slots, me, laid, OWN)
+    pump(FLIGHT + 2)
+    relay(1)
+    top_in[me] = top_part[mine, :]
+    for d in range(1, n):
+        share_copy(d).wait_recv()
+    total = top_in[0]
+    for s in range(1, n):
+        total += top_in[s]
+    top_own[mine, :] = total
+
+    @pl.when(is_inner)
+    def _():
+        ext_src_copy.wait_recv()
+        lay_ext(SIDE, 1, raw)
+        for at, to in enumerate((me, other)):
+            args = sub_in[to, pl.ds(end, 1)], ext_src[pl.ds(to, 1)], sub_in[to, pl.ds(n + end, 1)]
+            put_rows(at, ext_rows, args)
+
+    def top_copy(d):
+        return remote(top_own.at[mine], top_own.at[mine], top_sem, (d - 1,), sub_peer(d))
+
+    for d in range(1, n):
+        top_copy(d).start()
+
+    ext_copy_rows.start()
+    pump(FLIGHT + 3)
+    relay(2)
+    relay_back(0)
+    pump(FLIGHT + 4)
+    relay(3)
+    relay_back(1)
+    pump(FLIGHT + 5)
     for d in range(1, n):
         top_copy(d).wait_recv()
     for d in range(1, groups):
         all_copy(d).start()
     tops[group] = top_own[...]
 
+    relay(4)
+    relay_back(2)
+    pump(FLIGHT + 6)
+
+    for side in range(2):
+        @pl.when(sends_rim[side] & late_rim[side])
+        def _(side=side):
+            rim_copy(side).start()
+
+    relay(5)
+    relay_back(3)
+    relay(6)
+    relay_back(4)
+    relay(7)
+    relay_back(5)
+    ext_copy_rows.wait()
+    for side in range(2):
+        @pl.when(takes_ext[side])
+        def _(side=side):
+            ext_copy(side).wait_recv()
+            lay_ext(side, 2 * side, ext_in)
+
     @pl.when(is_inner)
     def _():
-        for p in range(PARTS):
-            raw_copy(SIDE, p).wait_recv()
-
-    for side in range(2):
-        @pl.when(sends_ext[side])
-        def _(side=side):
-            ext_copy(side).start()
-
-    @pl.when(is_inner)
-    def _():
-        compute(end, laid, END)
-
-    pump(FLIGHT + 2)
-    relay(FAR, 0)
-    compute(me, laid, OWN)
-    pump(FLIGHT + 3)
-    relay(FAR, 1)
-    pump(FLIGHT + 4)
-    relay(FAR, 2)
-    relay_back(0)
-    pump(FLIGHT + 5)
-    relay(FAR, 3)
-    relay_back(1)
-    pump(FLIGHT + 6)
-
+        compute(ext_slots, 1, laid_ext, SECOND, add=True)
+        for c in range(AHEAD):
+            other_copy(SECOND, c).start()
+
+    relay_back(6)
     for d in range(1, groups):
         all_copy(d).wait_recv()
     field = jnp.zeros((share, mid.shape[1]), F32)
@@ -633,20 +653,39 @@
     def field_copy(d):
         return remote(field_own.at[mine], field_own.at[mine], field_sem, (d - 1,), sub_peer(d))
 
-    relay(FAR, 4)
-    relay_back(2)
     for d in range(1, n):
         field_copy(d).start()
-    pump(FLIGHT + 7)
-    relay(FAR, 5)
-    relay_back(3)
-    pump(FLIGHT + 8)
-    relay(FAR, 6)
-    relay_back(4)
-    pump(FLIGHT + 9)
-    relay(FAR, 7)
-    relay_back(5)
-    pump(FLIGHT + 10)
+
+    @pl.when(is_inner)
+    def _():
+        for c in range(AHEAD, CHUNKS):
+            other_copy(SECOND, c).start()
+
+    relay_back(7)
+
+    @pl.when(is_inner)
+    def _():
+        compute(ext_slots, 0, laid_ext, OWN, add=True)
+
+    for side in range(2):
+        @pl.when(takes_rim[side])
+        def _(side=side):
+            rim_copy(side).wait_recv()
+
+    @pl.loop(0, halo)
+    def _(l):
+        lay_out(laid_near, l, rim[0, l])
+        lay_out(laid_near, halo + leaves + l, rim[1, l])
+
+    @pl.loop(0, leaves, unroll=2)
+    def _(l):
+        lay_out(laid_near, halo + l, cur[l])
+
+    near_copy.wait()
+    for p in range(PARTS):
+        block_load(p).wait()
+    in_order(near_slots, 0, near_count, near_product)
+    gather(near_slots, 0, put_near)
 
     for d in range(1, n):
         field_copy(d).wait_recv()
@@ -656,51 +695,15 @@
     def _(l):
         part[OWN, l] += dot3(transfer[l], mid[...])
 
-    relay(SECOND, 0)
-    relay_back(6)
-    pump(FLIGHT + 11)
-
-    def lay_ext(to, at, ref):
-        @pl.loop(0, leaves, unroll=2)
-        def _(l):
-            lay_out(laid_ext, at * leaves + l, ref[to, l])
-
-    @pl.when(is_inner)
-    def _():
-        lay_ext(SIDE, 1, raw)
-
-    relay(SECOND, 1)
-    relay_back(7)
-    pump(FLIGHT + 12)
-    for side in range(2):
-        @pl.when(takes_ext[side])
-        def _(side=side):
-            ext_copy(side).wait_recv()
-            lay_ext(side, 2 * side, ext_in)
-
-    relay(SECOND, 2)
-    pump(FLIGHT + 13)
-
-    @pl.when(is_inner)
-    def _():
-        compute(n, laid_ext, OWN, add=True)
-
     def finish(c):
-        other_copy(1, c).wait_recv()
+        other_copy(SECOND, c).wait_recv()
         for i in range(per):
             l = c * per + i
-            field = part[OWN, l] + from_other[1, l]
+            field = part[OWN, l] + from_other[SECOND, l]
             out[l] = dot3(masked(basis[l], rank[l]), field) + near_part[l]
 
-    relay(SECOND, 3)
-    pump(FLIGHT + 14)
-    done = 0
-    for c in range(4, CHUNKS + 2):
-        if c < CHUNKS:
-            relay(SECOND, c)
-        while done <= c - 2:
-            finish(done)
-            done += 1
+    for c in range(CHUNKS):
+        finish(c)
 
     for side in range(2):
         @pl.when(sends_rim[side])
@@ -734,14 +737,15 @@
     def _():
         for c in range(CHUNKS):
             other_copy(FAR, c).wait_send()
+            back_copy(c).wait_send()
+        for c in range(CHUNKS):
             other_copy(SECOND, c).wait_send()
-            back_copy(c).wait_send()
 
     @pl.when(is_end)
     def _():
         ext_src_copy.wait_send()
-        for item in items[-FLIGHT:]:
-            end_copy(*item).wait_send()
+        for c in range(CHUNKS - FLIGHT, CHUNKS):
+            end_copy(c).wait_send()
 
 
 def fields(count, partner, rank, numbers, shares, coupling, cur, basis, transfer, blocks, table):
@@ -755,7 +759,7 @@
     b16 = lambda *shape: pltpu.VMEM(shape, BF16)
     block = lambda *lead: f32(*lead, width, cols)
     dma = lambda *shape: pltpu.SemaphoreType.DMA(shape)
-    lists = 4 * (n + 1)
+    lists = 4 * n
     lists = -(-lists // 8) * 8
     return pl.pallas_call(
         functools.partial(field_kernel, count),
@@ -776,9 +780,10 @@
             block(2, HALO_L),
             b16(3 * leaves, 2 * width, 2 * cols),
             b16(3 * leaves, 2 * width, 2 * cols),
+            b16(leaves + 2 * HALO_L, 2 * width, 2 * cols),
             block(max(count, blocks.shape[0])),
             block(4, leaves),
-            block(2, leaves),
+            block(leaves),
             block(2, leaves),
             block(leaves),
             f32(width, width),
@@ -796,12 +801,14 @@
             i32(8, 128),
             i32(8, 128),
             i32(lists, 128),
+            i32(8, 128),
             pltpu.SMEM((8, 128), jnp.int32),
             pltpu.SMEM((lists, 128), jnp.int32),
+            pltpu.SMEM((8, 128), jnp.int32),
             dma(3, PARTS),
             dma(PARTS),
             dma(PARTS),
-            dma(2),
+            dma(3),
             dma(2, 2),
             dma(2, n - 1),
             dma(2, 2),
@@ -814,7 +821,7 @@
             dma(2, groups - 1),
             dma(2, n - 1),
             dma(2, CHUNKS),
-            dma(2, CHUNKS),
+            dma(CHUNKS),
             dma(2, CHUNKS),
             dma(CHUNKS),
         ],

time: 109 us -> 95.7 us (0.88)
  the two profiles are of different devices: /device:TPU:14 before, /device:TPU:19 now
where the time goes in v1:
time: 95.7 us; the launch traced here: 95.5 us
  Pallas kernels  93.2 us (97%)
  local copies, waits for them, and re-layouts  2.26 us (2%)
    pallas_call x1, Pallas kernels, fields(): pl.pallas_call(functools.partial(field_kernel, count), in_specs=[SMEM] *...  93.2 us
    unnamed x1, local copies, waits for them, and re-layouts  2.26 us

profile of v1, /device:TPU:19, one launch (start us, length us, event | category | flops | bytes accessed | tf_op | source)
XLA Modules:
  0.0 95.5 jit_solution(8094274600507612018)
XLA Ops:
  0.0 93.2 %fields.1 = f32[16,128,128]{2,1,0:T(8,128)} custom-call(s32[4]{0:T(128)} %bitcast.17, s32[16]{0:T(128)} %rank.1, s32[3,4,12]{2,1,0:T(4,128)} %bitcast.14, s32[3,4,12]{2,1,0:T(4,128)} %bitcast.15, s32[3,4,12]{2,1,0:T(4,128)} %bitcast.16, s32[1,64]{1,0:T(1,128)} %near_tgt.1, s32[1,64]{1,0:T(1,128)} %near_src.1, f32[4,32,128]{2,1,0:T(8,128)} %bitcast.13, ...), custom_call_target="tpu_custom_call" | custom-call | flops 8153726976 | bytes 20971520 | tf_op jit(solution)/shard_map/fields/pallas_call | solution.py:764
  93.2 2.3 %copy.16 = f32[2048,128]{1,0:T(8,128)} copy(f32[2048,128]{1,0:T(8,128)} %bitcast.10) | data formatting | bytes 2097152

commit v2 on v1

--- a/solution.py
+++ b/solution.py
@@ -765,7 +765,7 @@
         functools.partial(field_kernel, count),
         in_specs=[SMEM] * 2 + [VMEM] * 7 + [ANY] * 5,
         out_specs=VMEM,
-        out_shape=jax.ShapeDtypeStruct((leaves, width, cols), F32),
+        out_shape=pltpu.VMEM((leaves, width, cols), F32),
         scratch_shapes=[
             block(leaves),
             f32(*basis.shape),
@@ -826,7 +826,7 @@
             dma(CHUNKS),
         ],
         compiler_params=pltpu.CompilerParams(
-            vmem_limit_bytes=67043328, collective_id=0, has_side_effects=True
+            vmem_limit_bytes=60 * 1024 * 1024, collective_id=0, has_side_effects=True
         ),
         cost_estimate=pl.CostEstimate(
             flops=int(9 * count * 12 * width * width * cols),

time: 95.7 us -> 93.3 us (0.975)
  local copies, waits for them, and re-layouts: 2.26 us -> 0.97 us
  Pallas kernels: 93.2 us -> 92.2 us
    unnamed x1, local copies, waits for them, and re-layouts: 2.26 us -> 0.97 us
    pallas_call x1, Pallas kernels: 93.2 us -> 92.2 us  [fields(): pl.pallas_call(functools.partial(field_kernel, count), in_specs=[SMEM] *...]
where the time goes in v2:
time: 93.3 us; the launch traced here: 93.2 us
  Pallas kernels  92.2 us (99%)
  local copies, waits for them, and re-layouts  0.97 us (1%)
    pallas_call x1, Pallas kernels, fields(): pl.pallas_call(functools.partial(field_kernel, count), in_specs=[SMEM] *...  92.2 us

profile of v2, /device:TPU:19, one launch (start us, length us, event | category | flops | bytes accessed | tf_op | source)
XLA Modules:
  0.0 93.2 jit_solution(959663470195051569)
XLA Ops:
  0.0 92.2 %fields.1 = f32[16,128,128]{2,1,0:T(8,128)S(1)} custom-call(s32[4]{0:T(128)} %bitcast.17, s32[16]{0:T(128)} %rank.1, s32[3,4,12]{2,1,0:T(4,128)} %bitcast.14, s32[3,4,12]{2,1,0:T(4,128)} %bitcast.15, s32[3,4,12]{2,1,0:T(4,128)} %bitcast.16, s32[1,64]{1,0:T(1,128)} %near_tgt.1, s32[1,64]{1,0:T(1,128)} %near_src.1, f32[4,32,128]{2,1,0:T(8,128)} %bitcast.13, ...), custom_call_target="tpu_custom_call" | custom-call | flops 8153726976 | bytes 20971520 | tf_op jit(solution)/shard_map/fields/pallas_call | solution.py:764
  92.2 1.0 %copy.16 = f32[2048,128]{1,0:T(8,128)} copy(f32[2048,128]{1,0:T(8,128)S(1)} %bitcast.10) | data formatting | bytes 2097152
